TPU v7x, 32 devices: a whole 2x2x4 slice. The times are simulated.
32 devices in a mesh: row: 8 (over y, x, core), col: 4 (over z).
Axes of the slice: x: 2, y: 2, z: 4, core: 2. Of those that a mesh axis runs over, the one named last changes fastest.
Arguments:
- signal: float32 [128, 128, 16, 256], P('row', 'col'), may hold values from -40 to 40, as said below
- start_frames: float32 [256, 32], replicated, may hold values from -6 to 6
- start_sends: float32 [16, 8], replicated, may hold values from -6 to 6
- start_rows: float32 [128, 64], replicated, may hold values from -6 to 6
- start_cols: float32 [128, 64], replicated, may hold values from -6 to 6
- rank_frames: int32 [1], replicated, may hold values from 16 to 32
- rank_sends: int32 [1], replicated, may hold values from 4 to 8
Outputs:
- filtered: float32 [128, 128, 16, 256], P('row', 'col')
Inputs may be any that keep to these rules, and one draw needn't show every extreme that they name: `signal`: beamformed samples.
All inputs are finite; a program needn't handle non-finite values.
Results may differ from a plain program's by a relative error of at most 0.0003.
Values sent between devices are 32-bit elements; how exact they have to be, the bound alone decides.
No kernel may reach another device: no remote copies, remote signals or barrier semaphores. Data moves between devices by JAX's collectives and lax.ppermute only.
A program may use at most 128 MiB of HBM per device.

v0:
```python
import jax
import jax.numpy as jnp
from jax import lax
from jax.sharding import PartitionSpec as P

NT = 256
NK = 16
TMAX = 32
KMAX = 8
RS = 64
ITERS = 2
CORE_W = 256


def orthonormal(gram, start):
    high = lax.Precision.HIGHEST
    basis = start
    for rounds in range(ITERS):
        image = jnp.dot(gram, basis, precision=high)
        inner = jnp.dot(image.T, image, precision=high)
        factor = jnp.linalg.cholesky(inner)
        basis = jax.scipy.linalg.solve_triangular(factor, image.T, lower=True).T
    return basis


def local(signal, start_frames, start_sends, start_rows, start_cols, rank_frames, rank_sends):
    high = lax.Precision.HIGHEST
    rows_dev, cols_dev = (signal.shape[0], signal.shape[1])
    pixels = rows_dev * cols_dev
    flattened = signal.reshape(-1, NT)
    blocks = signal.reshape(pixels, NK, NT)
    local_frames = jnp.einsum("pt,pu->tu", flattened, flattened, precision=high)
    local_sends = jnp.einsum("pkt,pjt->kj", blocks, blocks, precision=high)
    gram_frames, gram_sends = lax.psum((local_frames, local_sends), ("row", "col"))
    keep_frames = (jnp.arange(TMAX, dtype=jnp.int32) < rank_frames[0]).astype(jnp.float32)
    keep_sends = (jnp.arange(KMAX, dtype=jnp.int32) < rank_sends[0]).astype(jnp.float32)
    basis_frames = orthonormal(gram_frames, start_frames) * keep_frames[None, :]
    basis_sends = orthonormal(gram_sends, start_sends) * keep_sends[None, :]
    reduced = jnp.dot(flattened, basis_frames, precision=high).reshape(pixels, NK, TMAX)
    core = jnp.einsum("pkb,ka->pab", reduced, basis_sends, precision=high)
    core = core.reshape(rows_dev, cols_dev, CORE_W)
    gathered = lax.all_gather(core, "row", axis=0, tiled=True)
    total_rows = gathered.shape[0]
    unfolded = gathered.reshape(total_rows, -1)
    local_rows = jnp.dot(unfolded, unfolded.T, precision=high)
    gram_rows = lax.psum(local_rows, "col")
    basis_rows = orthonormal(gram_rows, start_rows)
    second = jnp.dot(basis_rows.T, unfolded, precision=high).reshape(RS, cols_dev, CORE_W)
    width = CORE_W // lax.axis_size("row")
    own_slice = lax.dynamic_slice_in_dim(second, lax.axis_index("row") * width, width, 2)
    across = lax.all_gather(own_slice, "col", axis=1, tiled=True)
    local_cols = jnp.einsum("sce,sde->cd", across, across, precision=high)
    gram_cols = lax.psum(local_cols, "row")
    basis_cols = orthonormal(gram_cols, start_cols)
    third_slice = jnp.einsum("cu,sce->sue", basis_cols, across, precision=high)
    third = lax.all_gather(third_slice, "row", axis=2, tiled=True)
    cols_own = lax.dynamic_slice_in_dim(basis_cols, lax.axis_index("col") * cols_dev, cols_dev, 0)
    rows_own = lax.dynamic_slice_in_dim(basis_rows, lax.axis_index("row") * rows_dev, rows_dev, 0)
    back_cols = jnp.einsum("cu,sue->sce", cols_own, third, precision=high)
    tissue_core = jnp.dot(rows_own, back_cols.reshape(RS, -1), precision=high)
    tissue_core = tissue_core.reshape(pixels, KMAX, TMAX)
    expanded = jnp.einsum("pab,ka->pkb", tissue_core, basis_sends, precision=high)
    tissue = jnp.dot(expanded.reshape(-1, TMAX), basis_frames.T, precision=high).reshape(
        signal.shape
    )
    return signal - tissue


def solution(mesh):
    return jax.shard_map(
        local,
        mesh=mesh,
        in_specs=(P("row", "col", None, None), P(), P(), P(), P(), P(), P()),
        out_specs=P("row", "col", None, None),
        check_vma=False,
    )
```

profile of v0, /device:TPU:0, one launch (start us, length us, event | category | flops | bytes accessed | tf_op | source)
XLA Modules:
  0.0 528.9 jit_solution(3371056779634263745)
XLA Ops:
  6.5 17.7 %convolution_bitcast_fusion.4 = f32[256,256]{1,0:T(8,128)} fusion(f32[16,32,16,256]{3,2,1,0:T(8,128)} %param.16), kind=kOutput, calls=%fused_computation.9 | convolution fusion | flops 6442450944 | bytes 8650752 | tf_op jit(solution)/shard_map/pt,pu->tu/dot_general | solution.py:32
  24.3 14.1 %convolution_bitcast_fusion.6 = f32[16,16]{1,0:T(8,128)S(1)} fusion(f32[16,32,16,256]{3,2,1,0:T(8,128)} %param.16), kind=kOutput, calls=%fused_computation.13 | convolution fusion | flops 402653184 | bytes 8389632 | tf_op jit(solution)/shard_map/pkt,pjt->kj/dot_general | solution.py:33
  39.8 42.4 %psum.28 = f32[16,16]{1,0:T(8,128)S(1)} all-reduce(f32[16,16]{1,0:T(8,128)S(1)} %convolution_bitcast_fusion.6), channel_id=1, replica_groups=mesh['row'=8,'col'=4] {'row','col'}, use_global_device_ids=true, to_apply=%region_0.0 | all-reduce | flops 256 | bytes 2048 | tf_op jit(solution)/shard_map/psum | solution.py:34
  88.6 65.3 %all-reduce.4.cloned.1.call-done = f32[256,256]{1,0:T(8,128)} async-done(((f32[256,256]{1,0:T(8,128)}), f32[256,256]{1,0:T(8,128)}) %all-reduce.4.cloned.1.call-update) | async-done | bytes 262160 | tf_op jit(solution)/shard_map/psum | solution.py:34
  170.9 9.9 %convolution_bitcast_fusion = f32[8192,32]{0,1:T(8,128)S(1)} fusion(f32[32,256]{1,0:T(8,128)S(1)} %convolution_multiply_fusion, f32[8192,256]{1,0:T(8,128)} %bitcast.199), kind=kOutput, calls=%fused_computation | convolution fusion | flops 805306368 | bytes 9469952 | tf_op jit(solution)/shard_map/dot_general | solution.py:39
  190.2 35.5 %all-gather.4.cloned.1.call-done = f32[128,32,256]{2,0,1:T(8,128)} async-done(((f32[16,32,256]{2,0,1:T(8,128)}), f32[128,32,256]{2,0,1:T(8,128)}) %all-gather.4.cloned.1.call-update) | async-done | bytes 4194320 | tf_op jit(solution)/shard_map/all_gather | solution.py:42
  225.7 7.6 %convolution_bitcast_fusion.5 = f32[128,128]{1,0:T(8,128)} fusion(f32[128,32,256]{2,0,1:T(8,128)} %all-gather.4.cloned.1.call-done), kind=kOutput, calls=%fused_computation.11 | convolution fusion | flops 1610612736 | bytes 4259840 | tf_op jit(solution)/shard_map/dot_general | solution.py:45
  233.4 5.6 %copy.60 = f32[128,32,256]{0,2,1:T(8,128)} copy(f32[128,32,256]{2,0,1:T(8,128)} %all-gather.4.cloned.1.call-done) | data formatting | bytes 8388608 | tf_op jit(solution)/shard_map/all_gather | solution.py:42
  239.0 28.8 %all-reduce.6.cloned.1.call-done = f32[128,128]{1,0:T(8,128)} async-done(((f32[128,128]{1,0:T(8,128)}), f32[128,128]{1,0:T(8,128)}) %all-reduce.6.cloned.1.call-update) | async-done | bytes 65552 | tf_op jit(solution)/shard_map/psum | solution.py:46
  269.2 5.8 %cholesky.202 = f32[64,64]{1,0:T(8,128)S(1)} custom-call(f32[64,64]{1,0:T(8,128)S(1)} %fusion.32), custom_call_target="Cholesky" | custom-call | tf_op jit(solution)/shard_map/jit(cholesky)/cholesky | solution.py:21
  276.5 4.9 custom-call.24
  283.0 5.8 %cholesky.213 = f32[64,64]{1,0:T(8,128)S(1)} custom-call(f32[64,64]{1,0:T(8,128)S(1)} %fusion.28), custom_call_target="Cholesky" | custom-call | tf_op jit(solution)/shard_map/jit(cholesky)/cholesky | solution.py:21
  290.3 4.9 custom-call.25
  295.5 5.4 %fusion = f32[64,32,256]{0,2,1:T(8,128)S(1)} fusion(f32[128,32,256]{0,2,1:T(8,128)} %copy.60, f32[64,128]{1,0:T(8,128)S(1)} %fusion.25), kind=kOutput, calls=%fused_computation.1 | convolution fusion | flops 805306368 | bytes 6324224 | tf_op jit(solution)/shard_map/dot_general | solution.py:48
  302.2 45.0 %all-gather.6.cloned.1.call-done = f32[64,128,32]{0,2,1:T(8,128)} async-done(((f32[64,32,32]{0,2,1:T(8,128)}), f32[64,128,32]{0,2,1:T(8,128)}) %all-gather.6.cloned.1.call-update) | async-done | bytes 1048592 | tf_op jit(solution)/shard_map/all_gather | solution.py:51
  347.2 7.0 %fusion.4 = f32[128,128]{1,0:T(8,128)} fusion(f32[64,128,32]{0,2,1:T(8,128)} %all-gather.6.cloned.1.call-done), kind=kOutput, calls=%fused_computation.10 | convolution fusion | flops 402653184 | bytes 1114112 | tf_op jit(solution)/shard_map/sce,sde->cd/dot_general | solution.py:52
  357.4 49.1 %all-reduce.8.cloned.1.call-done = f32[128,128]{1,0:T(8,128)} async-done(((f32[128,128]{1,0:T(8,128)}), f32[128,128]{1,0:T(8,128)}) %all-reduce.8.cloned.1.call-update) | async-done | bytes 65552 | tf_op jit(solution)/shard_map/psum | solution.py:53
  407.8 5.8 %cholesky.224 = f32[64,64]{1,0:T(8,128)S(1)} custom-call(f32[64,64]{1,0:T(8,128)S(1)} %fusion.23), custom_call_target="Cholesky" | custom-call | tf_op jit(solution)/shard_map/jit(cholesky)/cholesky | solution.py:21
  415.0 4.9 custom-call.26
  421.5 5.8 %cholesky.235 = f32[64,64]{1,0:T(8,128)S(1)} custom-call(f32[64,64]{1,0:T(8,128)S(1)} %fusion.19), custom_call_target="Cholesky" | custom-call | tf_op jit(solution)/shard_map/jit(cholesky)/cholesky | solution.py:21
  428.7 4.9 custom-call.27
  435.8 53.8 %all-gather.8.cloned.1.call-done = f32[64,64,256]{1,2,0:T(8,128)} async-done(((f32[64,64,32]{1,2,0:T(8,128)}), f32[64,64,256]{1,2,0:T(8,128)}) %all-gather.8.cloned.1.call-update) | async-done | bytes 4194320 | tf_op jit(solution)/shard_map/all_gather | solution.py:56
  489.6 11.5 %fusion.13 = f32[64,256,32]{1,2,0:T(8,128)S(1)} fusion(f32[64,64,256]{1,2,0:T(8,128)} %all-gather.8.cloned.1.call-done, f32[64,128]{1,0:T(8,128)S(1)} %fusion.16, s32[]{:T(128)S(6)} %select_n.20), kind=kOutput, calls=%fused_computation.25 | convolution fusion | flops 402653184 | bytes 6324228 | tf_op jit(solution)/shard_map/cu,sue->sce/dot_general | solution.py:59
  510.0 11.8 %convolution_subtract_fusion = f32[16,32,16,256]{3,2,1,0:T(8,128)} fusion(f32[16,32,16,256]{3,2,1,0:T(8,128)} %param.16, f32[16,32,16,32]{3,2,1,0:T(8,128)} %bitcast.200, f32[32,256]{1,0:T(8,128)S(1)} %convolution_multiply_fusion), kind=kOutput, calls=%fused_computation.3 | convolution fusion | flops 807403520 | bytes 17858560 | tf_op jit(solution)/shard_map/dot_general | solution.py:63
  (111 shorter events, 60.0 us)
Async XLA Ops:
  6.5 147.4 %copy-start = (f32[256,32]{0,1:T(8,128)S(1)}, f32[256,32]{0,1:T(8,128)}, u32[]{:S(2)}) copy-start(f32[256,32]{0,1:T(8,128)} %param.17) | copy-start | bytes 98308
  6.5 147.4 %all-reduce.4.cloned.1.call-start = ((), (), s32[]{:S(2)}) async-start(), calls=%async_computation | async-start | bytes 524288 | tf_op jit(solution)/shard_map/psum | solution.py:34
  24.3 57.9 %copy-start.4 = (f32[16,8]{0,1:T(8,128)S(1)}, f32[16,8]{0,1:T(8,128)}, u32[]{:S(2)}) copy-start(f32[16,8]{0,1:T(8,128)} %param.18) | copy-start | bytes 1540
  24.3 201.5 %all-gather.4.cloned.1.call-start = ((), (), s32[]{:S(2)}) async-start(), calls=%async_computation.1 | async-start | bytes 4718592 | tf_op jit(solution)/shard_map/all_gather | solution.py:42
  189.9 77.9 %all-reduce.6.cloned.1.call-start = ((), (), s32[]{:S(2)}) async-start(), calls=%async_computation.2 | async-start | bytes 131072 | tf_op jit(solution)/shard_map/psum | solution.py:46
  233.3 113.9 %all-gather.6.cloned.1.call-start = ((), (), s32[]{:S(2)}) async-start(), calls=%async_computation.3 | async-start | bytes 2621440 | tf_op jit(solution)/shard_map/all_gather | solution.py:51
  233.4 34.4 %copy-start.2 = (f32[128,64]{0,1:T(8,128)S(1)}, f32[128,64]{0,1:T(8,128)}, u32[]{:S(2)}) copy-start(f32[128,64]{0,1:T(8,128)} %param.19) | copy-start | bytes 98308
  300.9 105.6 %copy-start.3 = (f32[128,64]{0,1:T(8,128)S(1)}, f32[128,64]{0,1:T(8,128)}, u32[]{:S(2)}) copy-start(f32[128,64]{0,1:T(8,128)} %param.20) | copy-start | bytes 98308
  301.7 104.7 %all-reduce.8.cloned.1.call-start = ((), (), s32[]{:S(2)}) async-start(), calls=%async_computation.4 | async-start | bytes 131072 | tf_op jit(solution)/shard_map/psum | solution.py:53
  354.3 135.3 %all-gather.8.cloned.1.call-start = ((), (), s32[]{:S(2)}) async-start(), calls=%async_computation.5 | async-start | bytes 9437184 | tf_op jit(solution)/shard_map/all_gather | solution.py:56
  510.0 11.8 %copy-start.1 = (f32[256,32]{0,1:T(8,128)S(1)}, f32[256,32]{0,1:T(8,128)}, u32[]{:S(2)}) copy-start(f32[256,32]{0,1:T(8,128)} %param.17) | copy-start | bytes 98308
Sparse Core Ops, SparseCore 0:
  24.4 129.5 all-reduce.3
  190.1 35.6 all-gather.3
  233.5 34.2 all-reduce.5
  301.9 45.3 all-gather.5
  354.4 51.9 all-reduce.7
  435.9 53.6 all-gather.7
where the time goes:
time: 537 us; the launch traced here: 529 us
  waiting for transfers between devices  278 us (52%)
  matrix products  100 us (19%)
  other arithmetic  67.3 us (13%)
  blocking collectives  42.4 us (8%)
  local copies, waits for them, and re-layouts  25.1 us (5%)
  between operations  15.5 us (3%)
    psum x1, waiting for transfers between devices, local(): lax.psum((local_frames, local_sends), ('row', 'col'))  65.3 us
    all_gather x1, waiting for transfers between devices, local(): third = lax.all_gather(third_slice, 'row', axis=2, tiled=True)  53.8 us
    psum x1, waiting for transfers between devices, local(): gram_cols = lax.psum(local_cols, 'row')  49.1 us
    all_gather x1, waiting for transfers between devices, local(): across = lax.all_gather(own_slice, 'col', axis=1, tiled=True)  45 us
    psum x1, blocking collectives, local(): lax.psum((local_frames, local_sends), ('row', 'col'))  42.4 us
    another operation x24, other arithmetic, orthonormal(): factor = jnp.linalg.cholesky(inner)  36.3 us
    all_gather x1, waiting for transfers between devices, local(): gathered = lax.all_gather(core, 'row', axis=0, tiled=True)  35.5 us
    another operation x16, other arithmetic, orthonormal(): basis = jax.scipy.linalg.solve_triangular(factor, image.T, lower=True).T  31 us
  transfers between devices with their start and end apart: 6, of which 6 were waited for; matrix products, arithmetic and copies ran while one was open for 6% of the time, Pallas kernels for 0%

commit v1 on v0

--- a/solution.py
+++ b/solution.py
@@ -50,7 +50,13 @@
     own_slice = lax.dynamic_slice_in_dim(second, lax.axis_index("row") * width, width, 2)
     across = lax.all_gather(own_slice, "col", axis=1, tiled=True)
     local_cols = jnp.einsum("sce,sde->cd", across, across, precision=high)
-    gram_cols = lax.psum(local_cols, "row")
+    count = lax.axis_size("row")
+    gram_cols, reach = (local_cols, 1)
+    while reach < count:
+        gram_cols = gram_cols + lax.ppermute(
+            gram_cols, "row", [(i, i ^ reach) for i in range(count)]
+        )
+        reach = 2 * reach
     basis_cols = orthonormal(gram_cols, start_cols)
     third_slice = jnp.einsum("cu,sce->sue", basis_cols, across, precision=high)
     third = lax.all_gather(third_slice, "row", axis=2, tiled=True)

time: 537 us -> 492 us (0.916)
  waiting for transfers between devices: 278 us -> 232 us
    psum x1 -> x0, waiting for transfers between devices: 49.1 us -> none  [local(): gram_cols = lax.psum(local_cols, 'row')]
  transfers between devices with their start and end apart: 6 -> 8, of which waited for: 6 -> 7; matrix products, arithmetic and copies ran while one was open for 6% -> 6% of each run, Pallas kernels for 0% -> 0%
where the time goes in v1:
time: 492 us; the launch traced here: 484 us
  waiting for transfers between devices  232 us (47%)
  matrix products  97.8 us (20%)
  other arithmetic  67.4 us (14%)
  blocking collectives  42.4 us (9%)
  local copies, waits for them, and re-layouts  25.1 us (5%)
  between operations  15.2 us (3%)
    psum x1, waiting for transfers between devices, local(): lax.psum((local_frames, local_sends), ('row', 'col'))  65.3 us
    all_gather x1, waiting for transfers between devices, local(): third = lax.all_gather(third_slice, 'row', axis=2, tiled=True)  53 us
    all_gather x1, waiting for transfers between devices, local(): across = lax.all_gather(own_slice, 'col', axis=1, tiled=True)  45 us
    psum x1, blocking collectives, local(): lax.psum((local_frames, local_sends), ('row', 'col'))  42.4 us
    another operation x24, other arithmetic, orthonormal(): factor = jnp.linalg.cholesky(inner)  36.3 us
    all_gather x1, waiting for transfers between devices, local(): gathered = lax.all_gather(core, 'row', axis=0, tiled=True)  35.5 us
    another operation x16, other arithmetic, orthonormal(): basis = jax.scipy.linalg.solve_triangular(factor, image.T, lower=True).T  31 us
    psum x1, waiting for transfers between devices, local(): gram_rows = lax.psum(local_rows, 'col')  28.8 us
  transfers between devices with their start and end apart: 8, of which 7 were waited for; matrix products, arithmetic and copies ran while one was open for 6% of the time, Pallas kernels for 0%

profile of v1, /device:TPU:0, one launch (start us, length us, event | category | flops | bytes accessed | tf_op | source)
XLA Modules:
  0.0 483.6 jit_solution(12612667114300696734)
XLA Ops:
  6.5 17.7 %convolution_bitcast_fusion.4 = f32[256,256]{1,0:T(8,128)} fusion(f32[16,32,16,256]{3,2,1,0:T(8,128)} %param.16), kind=kOutput, calls=%fused_computation.9 | convolution fusion | flops 6442450944 | bytes 8650752 | tf_op jit(solution)/shard_map/pt,pu->tu/dot_general | solution.py:32
  24.3 14.1 %convolution_bitcast_fusion.6 = f32[16,16]{1,0:T(8,128)S(1)} fusion(f32[16,32,16,256]{3,2,1,0:T(8,128)} %param.16), kind=kOutput, calls=%fused_computation.13 | convolution fusion | flops 402653184 | bytes 8389632 | tf_op jit(solution)/shard_map/pkt,pjt->kj/dot_general | solution.py:33
  39.8 42.4 %psum.21 = f32[16,16]{1,0:T(8,128)S(1)} all-reduce(f32[16,16]{1,0:T(8,128)S(1)} %convolution_bitcast_fusion.6), channel_id=1, replica_groups=mesh['row'=8,'col'=4] {'row','col'}, use_global_device_ids=true, to_apply=%region_0.0 | all-reduce | flops 256 | bytes 2048 | tf_op jit(solution)/shard_map/psum | solution.py:34
  88.6 65.3 %all-reduce.3.cloned.1.call-done = f32[256,256]{1,0:T(8,128)} async-done(((f32[256,256]{1,0:T(8,128)}), f32[256,256]{1,0:T(8,128)}) %all-reduce.3.cloned.1.call-update) | async-done | bytes 262160 | tf_op jit(solution)/shard_map/psum | solution.py:34
  170.9 9.9 %convolution_bitcast_fusion = f32[8192,32]{0,1:T(8,128)S(1)} fusion(f32[32,256]{1,0:T(8,128)S(1)} %convolution_multiply_fusion, f32[8192,256]{1,0:T(8,128)} %bitcast.199), kind=kOutput, calls=%fused_computation | convolution fusion | flops 805306368 | bytes 9469952 | tf_op jit(solution)/shard_map/dot_general | solution.py:39
  190.2 35.5 %all-gather.4.cloned.1.call-done = f32[128,32,256]{2,0,1:T(8,128)} async-done(((f32[16,32,256]{2,0,1:T(8,128)}), f32[128,32,256]{2,0,1:T(8,128)}) %all-gather.4.cloned.1.call-update) | async-done | bytes 4194320 | tf_op jit(solution)/shard_map/all_gather | solution.py:42
  225.7 7.6 %convolution_bitcast_fusion.5 = f32[128,128]{1,0:T(8,128)} fusion(f32[128,32,256]{2,0,1:T(8,128)} %all-gather.4.cloned.1.call-done), kind=kOutput, calls=%fused_computation.11 | convolution fusion | flops 1610612736 | bytes 4259840 | tf_op jit(solution)/shard_map/dot_general | solution.py:45
  233.4 5.6 %copy.60 = f32[128,32,256]{0,2,1:T(8,128)} copy(f32[128,32,256]{2,0,1:T(8,128)} %all-gather.4.cloned.1.call-done) | data formatting | bytes 8388608 | tf_op jit(solution)/shard_map/all_gather | solution.py:42
  239.0 28.8 %all-reduce.5.cloned.1.call-done = f32[128,128]{1,0:T(8,128)} async-done(((f32[128,128]{1,0:T(8,128)}), f32[128,128]{1,0:T(8,128)}) %all-reduce.5.cloned.1.call-update) | async-done | bytes 65552 | tf_op jit(solution)/shard_map/psum | solution.py:46
  269.2 5.8 %cholesky.202 = f32[64,64]{1,0:T(8,128)S(1)} custom-call(f32[64,64]{1,0:T(8,128)S(1)} %fusion.32), custom_call_target="Cholesky" | custom-call | tf_op jit(solution)/shard_map/jit(cholesky)/cholesky | solution.py:21
  276.5 4.9 %custom-call.24 = f32[1,64,64]{1,2,0:T(8,128)S(1)} custom-call(f32[1,64,64]{2,1,0:T(8,128)S(1)} %fusion.8), custom_call_target="InvertDiagBlocksLowerTriangular" | custom-call | tf_op jit(solution)/shard_map/jit(_solve_triangular)/triangular_solve | solution.py:22
  283.0 5.8 %cholesky.213 = f32[64,64]{1,0:T(8,128)S(1)} custom-call(f32[64,64]{1,0:T(8,128)S(1)} %fusion.28), custom_call_target="Cholesky" | custom-call | tf_op jit(solution)/shard_map/jit(cholesky)/cholesky | solution.py:21
  290.3 4.9 %custom-call.25 = f32[1,64,64]{1,2,0:T(8,128)S(1)} custom-call(f32[1,64,64]{2,1,0:T(8,128)S(1)} %fusion.9), custom_call_target="InvertDiagBlocksLowerTriangular" | custom-call | tf_op jit(solution)/shard_map/jit(_solve_triangular)/triangular_solve | solution.py:22
  295.5 5.4 %fusion = f32[64,32,256]{0,2,1:T(8,128)S(1)} fusion(f32[128,32,256]{0,2,1:T(8,128)} %copy.60, f32[64,128]{1,0:T(8,128)S(1)} %fusion.25), kind=kOutput, calls=%fused_computation.1 | convolution fusion | flops 805306368 | bytes 6324224 | tf_op jit(solution)/shard_map/dot_general | solution.py:48
  302.2 45.0 %all-gather.6.cloned.1.call-done = f32[64,128,32]{0,2,1:T(8,128)} async-done(((f32[64,32,32]{0,2,1:T(8,128)}), f32[64,128,32]{0,2,1:T(8,128)}) %all-gather.6.cloned.1.call-update) | async-done | bytes 1048592 | tf_op jit(solution)/shard_map/all_gather | solution.py:51
  347.2 6.4 %fusion.4 = f32[128,128]{1,0:T(8,128)S(1)} fusion(f32[64,128,32]{0,2,1:T(8,128)} %all-gather.6.cloned.1.call-done), kind=kOutput, calls=%fused_computation.10 | convolution fusion | flops 402653184 | bytes 1114112 | tf_op jit(solution)/shard_map/sce,sde->cd/dot_general | solution.py:52
  364.4 5.8 %cholesky.224 = f32[64,64]{1,0:T(8,128)S(1)} custom-call(f32[64,64]{1,0:T(8,128)S(1)} %fusion.23), custom_call_target="Cholesky" | custom-call | tf_op jit(solution)/shard_map/jit(cholesky)/cholesky | solution.py:21
  371.6 4.9 %custom-call.26 = f32[1,64,64]{1,2,0:T(8,128)S(1)} custom-call(f32[1,64,64]{2,1,0:T(8,128)S(1)} %fusion.10), custom_call_target="InvertDiagBlocksLowerTriangular" | custom-call | tf_op jit(solution)/shard_map/jit(_solve_triangular)/triangular_solve | solution.py:22
  377.3 5.8 %cholesky.235 = f32[64,64]{1,0:T(8,128)S(1)} custom-call(f32[64,64]{1,0:T(8,128)S(1)} %fusion.19), custom_call_target="Cholesky" | custom-call | tf_op jit(solution)/shard_map/jit(cholesky)/cholesky | solution.py:21
  384.5 4.9 %custom-call.27 = f32[1,64,64]{1,2,0:T(8,128)S(1)} custom-call(f32[1,64,64]{2,1,0:T(8,128)S(1)} %fusion.11), custom_call_target="InvertDiagBlocksLowerTriangular" | custom-call | tf_op jit(solution)/shard_map/jit(_solve_triangular)/triangular_solve | solution.py:22
  391.6 53.0 %all-gather.8.cloned.1.call-done = f32[64,64,256]{1,2,0:T(8,128)} async-done(((f32[64,64,32]{1,2,0:T(8,128)}), f32[64,64,256]{1,2,0:T(8,128)}) %all-gather.8.cloned.1.call-update) | async-done | bytes 4194320 | tf_op jit(solution)/shard_map/all_gather | solution.py:62
  444.6 11.5 %fusion.13 = f32[64,256,32]{1,2,0:T(8,128)S(1)} fusion(f32[64,64,256]{1,2,0:T(8,128)} %all-gather.8.cloned.1.call-done, f32[64,128]{1,0:T(8,128)S(1)} %fusion.16, s32[]{:T(128)S(6)} %select_n.20), kind=kOutput, calls=%fused_computation.25 | convolution fusion | flops 402653184 | bytes 6324228 | tf_op jit(solution)/shard_map/cu,sue->sce/dot_general | solution.py:65
  461.1 3.8 copy.74
  464.9 11.8 %convolution_subtract_fusion = f32[16,32,16,256]{3,2,1,0:T(8,128)} fusion(f32[16,32,16,256]{3,2,1,0:T(8,128)} %param.16, f32[16,32,16,32]{3,2,1,0:T(8,128)} %bitcast.200, f32[32,256]{1,0:T(8,128)S(1)} %convolution_multiply_fusion), kind=kOutput, calls=%fused_computation.3 | convolution fusion | flops 807403520 | bytes 17858560 | tf_op jit(solution)/shard_map/dot_general | solution.py:69
  (117 shorter events, 61.6 us)
Async XLA Ops:
  6.5 147.4 %copy-start = (f32[256,32]{0,1:T(8,128)S(1)}, f32[256,32]{0,1:T(8,128)}, u32[]{:S(2)}) copy-start(f32[256,32]{0,1:T(8,128)} %param.17) | copy-start | bytes 98308
  6.5 147.4 %all-reduce.3.cloned.1.call-start = ((), (), s32[]{:S(2)}) async-start(), calls=%async_computation | async-start | bytes 524288 | tf_op jit(solution)/shard_map/psum | solution.py:34
  24.3 57.9 %copy-start.4 = (f32[16,8]{0,1:T(8,128)S(1)}, f32[16,8]{0,1:T(8,128)}, u32[]{:S(2)}) copy-start(f32[16,8]{0,1:T(8,128)} %param.18) | copy-start | bytes 1540
  24.3 201.5 %all-gather.4.cloned.1.call-start = ((), (), s32[]{:S(2)}) async-start(), calls=%async_computation.1 | async-start | bytes 4718592 | tf_op jit(solution)/shard_map/all_gather | solution.py:42
  189.9 77.9 %all-reduce.5.cloned.1.call-start = ((), (), s32[]{:S(2)}) async-start(), calls=%async_computation.2 | async-start | bytes 131072 | tf_op jit(solution)/shard_map/psum | solution.py:46
  233.3 113.9 %all-gather.6.cloned.1.call-start = ((), (), s32[]{:S(2)}) async-start(), calls=%async_computation.3 | async-start | bytes 2621440 | tf_op jit(solution)/shard_map/all_gather | solution.py:51
  233.4 34.4 %copy-start.2 = (f32[128,64]{0,1:T(8,128)S(1)}, f32[128,64]{0,1:T(8,128)}, u32[]{:S(2)}) copy-start(f32[128,64]{0,1:T(8,128)} %param.19) | copy-start | bytes 98308
  300.9 63.0 %copy-start.3 = (f32[128,64]{0,1:T(8,128)S(1)}, f32[128,64]{0,1:T(8,128)}, u32[]{:S(2)}) copy-start(f32[128,64]{0,1:T(8,128)} %param.20) | copy-start | bytes 98308
  301.7 142.9 %all-gather.8.cloned.1.call-start = ((), (), s32[]{:S(2)}) async-start(), calls=%async_computation.4 | async-start | bytes 9437184 | tf_op jit(solution)/shard_map/all_gather | solution.py:62
  353.6 1.3 collective-permute-start
  355.0 4.3 collective-permute-start.1
  359.3 4.6 collective-permute-start.2
  464.9 11.8 %copy-start.1 = (f32[256,32]{0,1:T(8,128)S(1)}, f32[256,32]{0,1:T(8,128)}, u32[]{:S(2)}) copy-start(f32[256,32]{0,1:T(8,128)} %param.17) | copy-start | bytes 98308
Sparse Core Ops, SparseCore 0:
  24.4 129.5 all-reduce.2
  190.1 35.6 all-gather.3
  233.5 34.2 all-reduce.4
  301.9 45.3 all-gather.5
  391.7 52.8 all-gather.7
